TPU v7x, 32 devices: a whole 2x2x4 slice. The times are simulated.
32 devices in a mesh: vocab: 8 (over y, x, core), seq: 4 (over z).
Axes of the slice: x: 2, y: 2, z: 4, core: 2. Of those that a mesh axis runs over, the one named last changes fastest.
Arguments:
- latent_vector: bfloat16 [32, 7168], P('vocab', 'seq'), may hold values from -400 to 400
- unembedding_matrix: bfloat16 [7168, 8192], P('seq', 'vocab'), may hold values from -0.0625 to 0.0625
- occurrence_tally: int32 [32, 8192], P(('seq', 'vocab')), may hold values from 0 to 2
- additive_offset_table: bfloat16 [32, 8192], P(('seq', 'vocab')), may hold values from 0 to 0.5
- recurrence_charge: float32 [32], P(('seq', 'vocab')), may hold values from 0.05 to 0.5
- appearance_charge: float32 [32], P(('seq', 'vocab')), may hold values from 0.6 to 1.5
- recurrence_divisor: float32 [32], P('seq'), may hold values from 1.05 to 1.6
- softening_divisor: float32 [32], P('seq'), may hold values from 0.5 to 1.5
- nucleus_share_limit: float32 [32], P('seq'), may hold values from 0.5 to 0.95
Outputs:
- penalized_logits: bfloat16 [32, 8192], P('seq', 'vocab')
- cutoff: float32 [32], P('seq')
Inputs may be any that keep to these rules, and one draw needn't show every extreme that they name: `appearance_charge`: each sequence's presence penalty exceeds every entry of its token bias.
All inputs are finite; a program needn't handle non-finite values.
Results may differ from a plain program's by a relative error of at most 0.0047.
Values may be sent and summed in bfloat16 or wider, within the bound.
No kernel may reach another device: no remote copies, remote signals or barrier semaphores. Data moves between devices by JAX's collectives and lax.ppermute only.
A program may use at most 64 MiB of HBM per device.

v0:
```python
import jax
import jax.numpy as jnp
from jax import lax
from jax.sharding import PartitionSpec as P

STEPS = 9
cutoff_span = 32.0


def per_device(
    latent_vector,
    unembedding_matrix,
    occurrence_tally,
    additive_offset_table,
    recurrence_charge,
    appearance_charge,
    recurrence_divisor,
    softening_divisor,
    nucleus_share_limit,
):
    count_float = occurrence_tally.astype(jnp.float32)
    offset = (
        additive_offset_table.astype(jnp.float32)
        - recurrence_charge[:, None] * count_float
        - appearance_charge[:, None] * (occurrence_tally > 0).astype(jnp.float32)
    ).astype(jnp.bfloat16)
    relaid = lax.all_to_all(offset, "vocab", split_axis=1, concat_axis=0, tiled=True)
    partial_logits = jnp.dot(
        lax.all_gather(latent_vector, "vocab", axis=0, tiled=True),
        unembedding_matrix,
        preferred_element_type=jnp.float32,
    )
    logits = lax.psum_scatter(partial_logits, "seq", scatter_dimension=0, tiled=True)
    seen_mask = relaid < 0
    factor = recurrence_divisor[:, None]
    discouraged_scores = jnp.where(
        seen_mask, jnp.where(logits > 0, logits / factor, logits * factor), logits
    ) + relaid.astype(jnp.float32)
    softened_scores = discouraged_scores / softening_divisor[:, None]
    largest_score = lax.pmax(jnp.max(softened_scores, axis=1), "vocab")
    exponential_values = jnp.exp(softened_scores - largest_score[:, None])
    row_total = lax.psum(jnp.sum(exponential_values, axis=1), "vocab")
    target = nucleus_share_limit * row_total
    start_bounds = (jnp.zeros_like(largest_score), jnp.ones_like(largest_score))
    fractions = jnp.arange(1, 8, dtype=jnp.float32)

    def refine(turn_index, bounds):
        lower_end, upper_end = bounds
        stride = (upper_end - lower_end) * 0.125
        probes = lower_end[:, None] + stride[:, None] * fractions[None, :]
        threshold_candidates = largest_score[:, None] - cutoff_span * probes
        inside = softened_scores[:, None, :] >= threshold_candidates[:, :, None]
        partial_mass = jnp.sum(jnp.where(inside, exponential_values[:, None, :], 0.0), axis=2)
        cumulative_shares = lax.psum(partial_mass, "vocab")
        below_count = jnp.sum((cumulative_shares < target[:, None]).astype(jnp.float32), axis=1)
        new_lower = lower_end + stride * below_count
        return (new_lower, new_lower + stride)

    lower_end, upper_end = lax.fori_loop(0, STEPS // 3, refine, start_bounds)
    return (discouraged_scores.astype(jnp.bfloat16), largest_score - cutoff_span * upper_end)


def solution(mesh):
    in_specs = (
        P("vocab", "seq"),
        P("seq", "vocab"),
        P(("seq", "vocab"), None),
        P(("seq", "vocab"), None),
        P(("seq", "vocab")),
        P(("seq", "vocab")),
        P("seq"),
        P("seq"),
        P("seq"),
    )
    out_specs = (P("seq", "vocab"), P("seq"))
    return jax.shard_map(
        per_device, mesh=mesh, in_specs=in_specs, out_specs=out_specs, check_vma=False
    )
```

profile of v0, /device:TPU:0, one launch (start us, length us, event | category | flops | bytes accessed | tf_op | source)
XLA Modules:
  0.0 110.7 jit_solution(10906374789269794412)
XLA Ops:
  7.2 0.0 copy-start
  7.2 0.0 copy-start.1
  7.2 0.0 copy-start.3
  7.2 0.0 copy-start.2
  7.2 0.0 copy-start.4
  7.2 0.0 reduce-scatter.2.cloned.1.call-start
  7.3 10.9 %all-gather = bf16[8,4,1792]{2,1,0:T(4,128)(2,1)S(1)} all-gather(bf16[1,4,1792]{2,1,0:T(4,128)(2,1)} %bitcast.19), channel_id=1, replica_groups=mesh['vocab'=8,'seq'=4] {'vocab'}, dimensions={0}, use_global_device_ids=true | all-gather | bytes 129024 | tf_op jit(solution)/shard_map/all_gather | solution.py:29
  18.2 3.4 %fusion.9 = f32[32,1024]{1,0:T(8,128)} fusion(bf16[32,1792]{1,0:T(8,128)(2,1)S(1)} %reshape.88, bf16[1792,1024]{1,0:T(8,128)(2,1)} %param.12), kind=kOutput, calls=%fused_computation.20 | convolution fusion | flops 117440512 | bytes 3915776 | tf_op jit(solution)/shard_map/dot_general | solution.py:28
  21.6 0.0 reduce-scatter.2.cloned.1.call-update
  23.0 0.1 fusion.5
  23.0 0.5 broadcast.112
  23.6 0.7 reduce
  24.3 0.6 reshape.89
  24.9 3.3 %all-to-all-start = ((bf16[8,2,512]{2,1,0:T(2,128)(2,1)}), bf16[8,2,512]{2,1,0:T(2,128)(2,1)S(1)}, u32[]{:S(2)}, u32[]{:S(2)}) async-start(bf16[8,2,512]{2,1,0:T(2,128)(2,1)} %reshape.89), calls=%async_computation | async-start | bytes 32768 | tf_op jit(solution)/shard_map/all_to_all | solution.py:27
  28.3 4.7 %all-to-all-done = bf16[8,2,512]{2,1,0:T(2,128)(2,1)S(1)} async-done(((bf16[8,2,512]{2,1,0:T(2,128)(2,1)}), bf16[8,2,512]{2,1,0:T(2,128)(2,1)S(1)}, u32[]{:S(2)}, u32[]{:S(2)}) %all-to-all-start) | async-done | bytes 16416 | tf_op jit(solution)/shard_map/all_to_all | solution.py:27
  33.0 8.5 %reduce-scatter.2.cloned.1.call-done = f32[8,1024]{1,0:T(8,128)} async-done(((f32[32,1024]{1,0:T(8,128)}), f32[8,1024]{1,0:T(8,128)}) %reduce-scatter.2.cloned.1.call-update) | async-done | bytes 32784 | tf_op jit(solution)/shard_map/reduce_scatter | solution.py:33
  41.5 0.0 copy-done.3
  41.5 1.6 %fusion.8 = (f32[8]{0:T(128)S(1)}, f32[8,1024]{1,0:T(8,128)S(1)}, bf16[8,1024]{1,0:T(8,128)(2,1)}) fusion(f32[8]{0:T(128)S(1)} %copy-done.2, f32[8,1024]{1,0:T(8,128)} %reduce-scatter.2.cloned.1.call-done, f32[8]{0:T(128)S(1)} %copy-done.3, bf16[1,8,1024]{2,0,1:T(2,128)(2,1)S(1)} %bitcast.17), kind=kLoop, calls=%fused_computation.19 | loop fusion | flops 90104 | bytes 98400 | tf_op jit(solution)/shard_map/reduce_max | solution.py:40
  43.1 11.8 %pmax.7 = f32[8]{0:T(128)S(1)} all-reduce(f32[8]{0:T(128)S(1)} %get-tuple-element.91), channel_id=1, replica_groups=mesh['vocab'=8,'seq'=4] {'vocab'}, use_global_device_ids=true, to_apply=%region_2.3 | all-reduce | flops 8 | bytes 64 | tf_op jit(solution)/shard_map/pmax | solution.py:40
  54.9 0.2 fusion.7
  55.1 11.9 %psum.14 = f32[8]{0:T(128)S(1)} all-reduce(f32[8]{0:T(128)S(1)} %get-tuple-element.89), channel_id=1, replica_groups=mesh['vocab'=8,'seq'=4] {'vocab'}, use_global_device_ids=true, to_apply=%region_4.5 | all-reduce | flops 8 | bytes 64 | tf_op jit(solution)/shard_map/psum | solution.py:42
  66.9 36.4 %while.13 = (s32[]{:T(128)}, f32[8]{0:T(128)S(1)}, f32[8]{0:T(128)S(1)}, f32[8,1024]{1,0:T(8,128)S(1)}, f32[8]{0:T(128)S(1)}, /*index=5*/f32[8,1024]{1,0:T(8,128)S(1)}, f32[8]{0:T(128)S(1)}, s32[]{:T(128)}, s32[]{:T(128)}) while((s32[]{:T(128)}, f32[8]{0:T(128)S(1)}, f32[8]{0:T(128)S(1)}, f32[8,1024]{1,0:T(8,128)S(1)}, ...), condition=%wide.region_9.10_spmd.clone, body=%wide.region_5.9_spmd.clone.sunk | while | flops 172482 | bytes 67487 | solution.py:59
  67.0 0.1 multiply_subtract_fusion.3
  67.0 0.2 select_reduce_fusion.2
  67.2 11.8 %psum.17 = f32[8,7]{0,1:T(8,128)S(1)} all-reduce(f32[8,7]{0,1:T(8,128)S(1)} %select_reduce_fusion.2), channel_id=1, replica_groups=mesh['vocab'=8,'seq'=4] {'vocab'}, use_global_device_ids=true, to_apply=%region_7.7 | all-reduce | flops 56 | bytes 448 | tf_op jit(solution)/shard_map/while/body/eval_jaxpr/psum | solution.py:54
  79.1 0.1 multiply_subtract_fusion.3
  79.2 0.2 select_reduce_fusion.2
  79.3 11.8 %psum.17 = f32[8,7]{0,1:T(8,128)S(1)} all-reduce(f32[8,7]{0,1:T(8,128)S(1)} %select_reduce_fusion.2), channel_id=1, replica_groups=mesh['vocab'=8,'seq'=4] {'vocab'}, use_global_device_ids=true, to_apply=%region_7.7 | all-reduce | flops 56 | bytes 448 | tf_op jit(solution)/shard_map/while/body/eval_jaxpr/psum | solution.py:54
  91.2 0.1 multiply_subtract_fusion.3
  91.3 0.2 select_reduce_fusion.2
  91.5 11.8 %psum.17 = f32[8,7]{0,1:T(8,128)S(1)} all-reduce(f32[8,7]{0,1:T(8,128)S(1)} %select_reduce_fusion.2), channel_id=1, replica_groups=mesh['vocab'=8,'seq'=4] {'vocab'}, use_global_device_ids=true, to_apply=%region_7.7 | all-reduce | flops 56 | bytes 448 | tf_op jit(solution)/shard_map/while/body/eval_jaxpr/psum | solution.py:54
  103.3 0.5 multiply_subtract_fusion.1
  (21 shorter events, 0.2 us)
Async XLA Ops:
  7.2 15.8 %copy-start = (s32[1,8192]{1,0:T(1,128)S(1)}, s32[1,8192]{1,0:T(1,128)}, u32[]{:S(2)}) copy-start(s32[1,8192]{1,0:T(1,128)} %param.13) | copy-start | bytes 98308
  7.2 15.8 %copy-start.1 = (bf16[1,8192]{1,0:T(2,128)(2,1)S(1)}, bf16[1,8192]{1,0:T(2,128)(2,1)}, u32[]{:S(2)}) copy-start(bf16[1,8192]{1,0:T(2,128)(2,1)} %param.14) | copy-start | bytes 49156
  7.2 34.3 %copy-start.3 = (f32[8]{0:T(128)S(1)}, f32[8]{0:T(128)}, u32[]{:S(2)}) copy-start(f32[8]{0:T(128)} %param.17) | copy-start | bytes 100
  7.2 34.3 %copy-start.2 = (f32[8]{0:T(128)S(1)}, f32[8]{0:T(128)}, u32[]{:S(2)}) copy-start(f32[8]{0:T(128)} %param.18) | copy-start | bytes 100
  7.2 59.7 %copy-start.4 = (f32[8]{0:T(128)S(1)}, f32[8]{0:T(128)}, u32[]{:S(2)}) copy-start(f32[8]{0:T(128)} %param.19) | copy-start | bytes 100
  7.2 34.3 %reduce-scatter.2.cloned.1.call-start = ((), (), s32[]{:S(2)}) async-start(), calls=%async_computation.2 | async-start | bytes 163840 | tf_op jit(solution)/shard_map/reduce_scatter | solution.py:33
  24.9 8.0 %all-to-all-start = ((bf16[8,2,512]{2,1,0:T(2,128)(2,1)}), bf16[8,2,512]{2,1,0:T(2,128)(2,1)S(1)}, u32[]{:S(2)}, u32[]{:S(2)}) async-start(bf16[8,2,512]{2,1,0:T(2,128)(2,1)} %reshape.89), calls=%async_computation | async-start | bytes 32768 | tf_op jit(solution)/shard_map/all_to_all | solution.py:27
Sparse Core Ops, SparseCore 0:
  21.8 19.6 reduce-scatter.1
where the time goes:
time: 111 us
  blocking collectives  70 us (63%)
  between operations  15.4 us (14%)
  waiting for transfers between devices  13.2 us (12%)
  other arithmetic  3.96 us (4%)
  matrix products  3.42 us (3%)
  starting transfers between devices  3.37 us (3%)
  local copies, waits for them, and re-layouts  1.2 us (1%)
    psum x3, blocking collectives, refine(): cumulative_shares = lax.psum(partial_mass, 'vocab')  35.4 us
    psum x1, blocking collectives, per_device(): row_total = lax.psum(jnp.sum(exponential_values, axis=1), 'vocab')  11.9 us
    pmax x1, blocking collectives, per_device(): largest_score = lax.pmax(jnp.max(softened_scores, axis=1), 'vocab')  11.8 us
    all_gather x1, blocking collectives, per_device(): lax.all_gather(latent_vector, 'vocab', axis=0, tiled=True)  10.9 us
    reduce_scatter x1, waiting for transfers between devices, per_device(): lax.psum_scatter(partial_logits, 'seq', scatter_dimension=0, tiled=True)  8.54 us
    all_to_all x1, waiting for transfers between devices, per_device(): lax.all_to_all(offset, 'vocab', split_axis=1, concat_axis=0, tiled=True)  4.67 us
    dot_general x1, matrix products, per_device(): jnp.dot(lax.all_gather(latent_vector, 'vocab', axis=0, tiled=True), unemb...  3.42 us
    all_to_all x1, starting transfers between devices, per_device(): lax.all_to_all(offset, 'vocab', split_axis=1, concat_axis=0, tiled=True)  3.34 us
  transfers between devices with their start and end apart: 2, of which 2 were waited for; matrix products, arithmetic and copies ran while one was open for 2% of the time, Pallas kernels for 0%

commit v1 on v0

--- a/solution.py
+++ b/solution.py
@@ -51,7 +51,12 @@
         threshold_candidates = largest_score[:, None] - cutoff_span * probes
         inside = softened_scores[:, None, :] >= threshold_candidates[:, :, None]
         partial_mass = jnp.sum(jnp.where(inside, exponential_values[:, None, :], 0.0), axis=2)
-        cumulative_shares = lax.psum(partial_mass, "vocab")
+        workers = lax.axis_size("vocab")
+        cumulative_shares = partial_mass
+        for nth in [
+            [(p, p ^ dev) for p in range(workers)] for dev in (1, 2, 4, 8, 16) if dev < workers
+        ]:
+            cumulative_shares = cumulative_shares + lax.ppermute(cumulative_shares, "vocab", nth)
         below_count = jnp.sum((cumulative_shares < target[:, None]).astype(jnp.float32), axis=1)
         new_lower = lower_end + stride * below_count
         return (new_lower, new_lower + stride)

time: 111 us -> 101 us (0.910)
  blocking collectives: 70 us -> 34.6 us
  waiting for transfers between devices: 13.2 us -> 34 us
  starting transfers between devices: 3.37 us -> 7.87 us
    psum x3 -> x0, blocking collectives: 35.4 us -> none  [refine(): cumulative_shares = lax.psum(partial_mass, 'vocab')]
    ppermute x0 -> x9, waiting for transfers between devices: none -> 20.8 us  [refine(): lax.ppermute(cumulative_shares, 'vocab', nth)]
    ppermute x0 -> x9, starting transfers between devices: none -> 4.5 us  [refine(): lax.ppermute(cumulative_shares, 'vocab', nth)]
  transfers between devices with their start and end apart: 2 -> 11, of which waited for: 2 -> 11; matrix products, arithmetic and copies ran while one was open for 2% -> 2% of each run, Pallas kernels for 0% -> 0%
where the time goes in v1:
time: 101 us
  blocking collectives  34.6 us (34%)
  waiting for transfers between devices  34 us (34%)
  between operations  15.4 us (15%)
  starting transfers between devices  7.87 us (8%)
  other arithmetic  3.98 us (4%)
  matrix products  3.42 us (3%)
  local copies, waits for them, and re-layouts  1.2 us (1%)
    ppermute x9, waiting for transfers between devices, refine(): lax.ppermute(cumulative_shares, 'vocab', nth)  20.8 us
    psum x1, blocking collectives, per_device(): row_total = lax.psum(jnp.sum(exponential_values, axis=1), 'vocab')  11.9 us
    pmax x1, blocking collectives, per_device(): largest_score = lax.pmax(jnp.max(softened_scores, axis=1), 'vocab')  11.8 us
    all_gather x1, blocking collectives, per_device(): lax.all_gather(latent_vector, 'vocab', axis=0, tiled=True)  10.9 us
    reduce_scatter x1, waiting for transfers between devices, per_device(): lax.psum_scatter(partial_logits, 'seq', scatter_dimension=0, tiled=True)  8.54 us
    all_to_all x1, waiting for transfers between devices, per_device(): lax.all_to_all(offset, 'vocab', split_axis=1, concat_axis=0, tiled=True)  4.67 us
    ppermute x9, starting transfers between devices, refine(): lax.ppermute(cumulative_shares, 'vocab', nth)  4.5 us
    dot_general x1, matrix products, per_device(): jnp.dot(lax.all_gather(latent_vector, 'vocab', axis=0, tiled=True), unemb...  3.42 us
  transfers between devices with their start and end apart: 11, of which 11 were waited for; matrix products, arithmetic and copies ran while one was open for 2% of the time, Pallas kernels for 0%

profile of v1, /device:TPU:0, one launch (start us, length us, event | category | flops | bytes accessed | tf_op | source)
XLA Modules:
  0.0 100.6 jit_solution(15620220102057839805)
XLA Ops:
  7.3 10.9 %all-gather = bf16[8,4,1792]{2,1,0:T(4,128)(2,1)S(1)} all-gather(bf16[1,4,1792]{2,1,0:T(4,128)(2,1)} %bitcast.19), channel_id=1, replica_groups=mesh['vocab'=8,'seq'=4] {'vocab'}, dimensions={0}, use_global_device_ids=true | all-gather | bytes 129024 | tf_op jit(solution)/shard_map/all_gather | solution.py:29
  18.2 3.4 %fusion.9 = f32[32,1024]{1,0:T(8,128)} fusion(bf16[32,1792]{1,0:T(8,128)(2,1)S(1)} %reshape.88, bf16[1792,1024]{1,0:T(8,128)(2,1)} %param.12), kind=kOutput, calls=%fused_computation.21 | convolution fusion | flops 117440512 | bytes 3915776 | tf_op jit(solution)/shard_map/dot_general | solution.py:28
  23.0 0.5 broadcast.112
  23.6 0.7 reduce
  24.3 0.6 reshape.89
  24.9 3.3 %all-to-all-start = ((bf16[8,2,512]{2,1,0:T(2,128)(2,1)}), bf16[8,2,512]{2,1,0:T(2,128)(2,1)S(1)}, u32[]{:S(2)}, u32[]{:S(2)}) async-start(bf16[8,2,512]{2,1,0:T(2,128)(2,1)} %reshape.89), calls=%async_computation | async-start | bytes 32768 | tf_op jit(solution)/shard_map/all_to_all | solution.py:27
  28.3 4.7 %all-to-all-done = bf16[8,2,512]{2,1,0:T(2,128)(2,1)S(1)} async-done(((bf16[8,2,512]{2,1,0:T(2,128)(2,1)}), bf16[8,2,512]{2,1,0:T(2,128)(2,1)S(1)}, u32[]{:S(2)}, u32[]{:S(2)}) %all-to-all-start) | async-done | bytes 16416 | tf_op jit(solution)/shard_map/all_to_all | solution.py:27
  33.0 8.5 %reduce-scatter.2.cloned.1.call-done = f32[8,1024]{1,0:T(8,128)} async-done(((f32[32,1024]{1,0:T(8,128)}), f32[8,1024]{1,0:T(8,128)}) %reduce-scatter.2.cloned.1.call-update) | async-done | bytes 32784 | tf_op jit(solution)/shard_map/reduce_scatter | solution.py:33
  41.5 1.6 %fusion.8 = (f32[8]{0:T(128)S(1)}, f32[8,1024]{1,0:T(8,128)S(1)}, bf16[8,1024]{1,0:T(8,128)(2,1)}) fusion(f32[8]{0:T(128)S(1)} %copy-done.2, f32[8,1024]{1,0:T(8,128)} %reduce-scatter.2.cloned.1.call-done, f32[8]{0:T(128)S(1)} %copy-done.3, bf16[1,8,1024]{2,0,1:T(2,128)(2,1)S(1)} %bitcast.17), kind=kLoop, calls=%fused_computation.20 | loop fusion | flops 90104 | bytes 98400 | tf_op jit(solution)/shard_map/reduce_max | solution.py:40
  43.1 11.8 %pmax.7 = f32[8]{0:T(128)S(1)} all-reduce(f32[8]{0:T(128)S(1)} %get-tuple-element.91), channel_id=1, replica_groups=mesh['vocab'=8,'seq'=4] {'vocab'}, use_global_device_ids=true, to_apply=%region_2.3 | all-reduce | flops 8 | bytes 64 | tf_op jit(solution)/shard_map/pmax | solution.py:40
  54.9 0.2 fusion.7
  55.1 11.9 %psum.7 = f32[8]{0:T(128)S(1)} all-reduce(f32[8]{0:T(128)S(1)} %get-tuple-element.89), channel_id=1, replica_groups=mesh['vocab'=8,'seq'=4] {'vocab'}, use_global_device_ids=true, to_apply=%region_4.5 | all-reduce | flops 8 | bytes 64 | tf_op jit(solution)/shard_map/psum | solution.py:42
  66.9 26.3 %while.13 = (s32[]{:T(128)}, f32[8]{0:T(128)S(1)}, f32[8]{0:T(128)S(1)}, f32[8,1024]{1,0:T(8,128)S(1)}, f32[8]{0:T(128)S(1)}, /*index=5*/f32[8,1024]{1,0:T(8,128)S(1)}, f32[8]{0:T(128)S(1)}, s32[]{:T(128)}, s32[]{:T(128)}) while((s32[]{:T(128)}, f32[8]{0:T(128)S(1)}, f32[8]{0:T(128)S(1)}, f32[8,1024]{1,0:T(8,128)S(1)}, ...), condition=%wide.region_8.9_spmd.clone, body=%wide.region_5.8_spmd.clone.sunk | while | flops 172594 | bytes 71415 | solution.py:64
  67.0 0.1 multiply_subtract_fusion.3
  67.1 0.2 select_reduce_fusion.2
  67.3 1.2 %collective-permute-done = f32[8,7]{0,1:T(8,128)S(1)} collective-permute-done((f32[8,7]{0,1:T(8,128)S(1)}, f32[8,7]{0,1:T(8,128)S(1)}, u32[]{:S(2)}, u32[]{:S(2)}) %collective-permute-start) | collective-permute-done | bytes 256 | tf_op jit(solution)/shard_map/while/body/eval_jaxpr/ppermute | solution.py:59
  68.5 3.6 %collective-permute-done.1 = f32[8,7]{0,1:T(8,128)S(1)} collective-permute-done((f32[8,7]{0,1:T(8,128)S(1)}, f32[8,7]{0,1:T(8,128)S(1)}, u32[]{:S(2)}, u32[]{:S(2)}) %collective-permute-start.1) | collective-permute-done | bytes 256 | tf_op jit(solution)/shard_map/while/body/eval_jaxpr/ppermute | solution.py:59
  72.1 1.4 %collective-permute-start.2 = (f32[8,7]{0,1:T(8,128)S(1)}, f32[8,7]{0,1:T(8,128)S(1)}, u32[]{:S(2)}, u32[]{:S(2)}) collective-permute-start(f32[8,7]{0,1:T(8,128)S(1)} %add.81), channel_id=1, source_target_pairs={{0,16},{4,20},{8,24},{12,28},{16,0},{20,4},{24,8},{28,12},{1,17},{... | collective-permute-start | bytes 680 | tf_op jit(solution)/shard_map/while/body/eval_jaxpr/ppermute | solution.py:59
  73.5 2.2 %collective-permute-done.2 = f32[8,7]{0,1:T(8,128)S(1)} collective-permute-done((f32[8,7]{0,1:T(8,128)S(1)}, f32[8,7]{0,1:T(8,128)S(1)}, u32[]{:S(2)}, u32[]{:S(2)}) %collective-permute-start.2) | collective-permute-done | bytes 256 | tf_op jit(solution)/shard_map/while/body/eval_jaxpr/ppermute | solution.py:59
  75.8 0.1 multiply_subtract_fusion.3
  75.8 0.2 select_reduce_fusion.2
  76.1 1.2 %collective-permute-done = f32[8,7]{0,1:T(8,128)S(1)} collective-permute-done((f32[8,7]{0,1:T(8,128)S(1)}, f32[8,7]{0,1:T(8,128)S(1)}, u32[]{:S(2)}, u32[]{:S(2)}) %collective-permute-start) | collective-permute-done | bytes 256 | tf_op jit(solution)/shard_map/while/body/eval_jaxpr/ppermute | solution.py:59
  77.2 3.6 %collective-permute-done.1 = f32[8,7]{0,1:T(8,128)S(1)} collective-permute-done((f32[8,7]{0,1:T(8,128)S(1)}, f32[8,7]{0,1:T(8,128)S(1)}, u32[]{:S(2)}, u32[]{:S(2)}) %collective-permute-start.1) | collective-permute-done | bytes 256 | tf_op jit(solution)/shard_map/while/body/eval_jaxpr/ppermute | solution.py:59
  80.8 1.4 %collective-permute-start.2 = (f32[8,7]{0,1:T(8,128)S(1)}, f32[8,7]{0,1:T(8,128)S(1)}, u32[]{:S(2)}, u32[]{:S(2)}) collective-permute-start(f32[8,7]{0,1:T(8,128)S(1)} %add.81), channel_id=1, source_target_pairs={{0,16},{4,20},{8,24},{12,28},{16,0},{20,4},{24,8},{28,12},{1,17},{... | collective-permute-start | bytes 680 | tf_op jit(solution)/shard_map/while/body/eval_jaxpr/ppermute | solution.py:59
  82.3 2.2 %collective-permute-done.2 = f32[8,7]{0,1:T(8,128)S(1)} collective-permute-done((f32[8,7]{0,1:T(8,128)S(1)}, f32[8,7]{0,1:T(8,128)S(1)}, u32[]{:S(2)}, u32[]{:S(2)}) %collective-permute-start.2) | collective-permute-done | bytes 256 | tf_op jit(solution)/shard_map/while/body/eval_jaxpr/ppermute | solution.py:59
  84.5 0.1 multiply_subtract_fusion.3
  84.6 0.2 select_reduce_fusion.2
  84.9 1.2 %collective-permute-done = f32[8,7]{0,1:T(8,128)S(1)} collective-permute-done((f32[8,7]{0,1:T(8,128)S(1)}, f32[8,7]{0,1:T(8,128)S(1)}, u32[]{:S(2)}, u32[]{:S(2)}) %collective-permute-start) | collective-permute-done | bytes 256 | tf_op jit(solution)/shard_map/while/body/eval_jaxpr/ppermute | solution.py:59
  86.0 3.6 %collective-permute-done.1 = f32[8,7]{0,1:T(8,128)S(1)} collective-permute-done((f32[8,7]{0,1:T(8,128)S(1)}, f32[8,7]{0,1:T(8,128)S(1)}, u32[]{:S(2)}, u32[]{:S(2)}) %collective-permute-start.1) | collective-permute-done | bytes 256 | tf_op jit(solution)/shard_map/while/body/eval_jaxpr/ppermute | solution.py:59
  89.6 1.4 %collective-permute-start.2 = (f32[8,7]{0,1:T(8,128)S(1)}, f32[8,7]{0,1:T(8,128)S(1)}, u32[]{:S(2)}, u32[]{:S(2)}) collective-permute-start(f32[8,7]{0,1:T(8,128)S(1)} %add.81), channel_id=1, source_target_pairs={{0,16},{4,20},{8,24},{12,28},{16,0},{20,4},{24,8},{28,12},{1,17},{... | collective-permute-start | bytes 680 | tf_op jit(solution)/shard_map/while/body/eval_jaxpr/ppermute | solution.py:59
  91.1 2.2 %collective-permute-done.2 = f32[8,7]{0,1:T(8,128)S(1)} collective-permute-done((f32[8,7]{0,1:T(8,128)S(1)}, f32[8,7]{0,1:T(8,128)S(1)}, u32[]{:S(2)}, u32[]{:S(2)}) %collective-permute-start.2) | collective-permute-done | bytes 256 | tf_op jit(solution)/shard_map/while/body/eval_jaxpr/ppermute | solution.py:59
  93.3 0.5 multiply_subtract_fusion.1
  (42 shorter events, 0.6 us)
Async XLA Ops:
  7.2 15.8 %copy-start = (s32[1,8192]{1,0:T(1,128)S(1)}, s32[1,8192]{1,0:T(1,128)}, u32[]{:S(2)}) copy-start(s32[1,8192]{1,0:T(1,128)} %param.13) | copy-start | bytes 98308
  7.2 15.8 %copy-start.1 = (bf16[1,8192]{1,0:T(2,128)(2,1)S(1)}, bf16[1,8192]{1,0:T(2,128)(2,1)}, u32[]{:S(2)}) copy-start(bf16[1,8192]{1,0:T(2,128)(2,1)} %param.14) | copy-start | bytes 49156
  7.2 34.3 %copy-start.3 = (f32[8]{0:T(128)S(1)}, f32[8]{0:T(128)}, u32[]{:S(2)}) copy-start(f32[8]{0:T(128)} %param.17) | copy-start | bytes 100
  7.2 34.3 %copy-start.2 = (f32[8]{0:T(128)S(1)}, f32[8]{0:T(128)}, u32[]{:S(2)}) copy-start(f32[8]{0:T(128)} %param.18) | copy-start | bytes 100
  7.2 59.7 %copy-start.4 = (f32[8]{0:T(128)S(1)}, f32[8]{0:T(128)}, u32[]{:S(2)}) copy-start(f32[8]{0:T(128)} %param.19) | copy-start | bytes 100
  7.2 34.3 %reduce-scatter.2.cloned.1.call-start = ((), (), s32[]{:S(2)}) async-start(), calls=%async_computation.2 | async-start | bytes 163840 | tf_op jit(solution)/shard_map/reduce_scatter | solution.py:33
  24.9 8.0 %all-to-all-start = ((bf16[8,2,512]{2,1,0:T(2,128)(2,1)}), bf16[8,2,512]{2,1,0:T(2,128)(2,1)S(1)}, u32[]{:S(2)}, u32[]{:S(2)}) async-start(bf16[8,2,512]{2,1,0:T(2,128)(2,1)} %reshape.89), calls=%async_computation | async-start | bytes 32768 | tf_op jit(solution)/shard_map/all_to_all | solution.py:27
  67.2 1.2 %collective-permute-start = (f32[8,7]{0,1:T(8,128)S(1)}, f32[8,7]{0,1:T(8,128)S(1)}, u32[]{:S(2)}, u32[]{:S(2)}) collective-permute-start(f32[8,7]{0,1:T(8,128)S(1)} %select_reduce_fusion.2), channel_id=1, source_target_pairs={{0,4},{4,0},{8,12},{12,8},{16,20},{20,16},{24,28},{28,24},{1,5},{5... | collective-permute-start | bytes 680 | tf_op jit(solution)/shard_map/while/body/eval_jaxpr/ppermute | solution.py:59
  68.5 3.6 %collective-permute-start.1 = (f32[8,7]{0,1:T(8,128)S(1)}, f32[8,7]{0,1:T(8,128)S(1)}, u32[]{:S(2)}, u32[]{:S(2)}) collective-permute-start(f32[8,7]{0,1:T(8,128)S(1)} %add.80), channel_id=1, source_target_pairs={{0,8},{4,12},{8,0},{12,4},{16,24},{20,28},{24,16},{28,20},{1,9},{5... | collective-permute-start | bytes 680 | tf_op jit(solution)/shard_map/while/body/eval_jaxpr/ppermute | solution.py:59
  72.1 3.6 %collective-permute-start.2 = (f32[8,7]{0,1:T(8,128)S(1)}, f32[8,7]{0,1:T(8,128)S(1)}, u32[]{:S(2)}, u32[]{:S(2)}) collective-permute-start(f32[8,7]{0,1:T(8,128)S(1)} %add.81), channel_id=1, source_target_pairs={{0,16},{4,20},{8,24},{12,28},{16,0},{20,4},{24,8},{28,12},{1,17},{... | collective-permute-start | bytes 680 | tf_op jit(solution)/shard_map/while/body/eval_jaxpr/ppermute | solution.py:59
  76.0 1.2 %collective-permute-start = (f32[8,7]{0,1:T(8,128)S(1)}, f32[8,7]{0,1:T(8,128)S(1)}, u32[]{:S(2)}, u32[]{:S(2)}) collective-permute-start(f32[8,7]{0,1:T(8,128)S(1)} %select_reduce_fusion.2), channel_id=1, source_target_pairs={{0,4},{4,0},{8,12},{12,8},{16,20},{20,16},{24,28},{28,24},{1,5},{5... | collective-permute-start | bytes 680 | tf_op jit(solution)/shard_map/while/body/eval_jaxpr/ppermute | solution.py:59
  77.2 3.6 %collective-permute-start.1 = (f32[8,7]{0,1:T(8,128)S(1)}, f32[8,7]{0,1:T(8,128)S(1)}, u32[]{:S(2)}, u32[]{:S(2)}) collective-permute-start(f32[8,7]{0,1:T(8,128)S(1)} %add.80), channel_id=1, source_target_pairs={{0,8},{4,12},{8,0},{12,4},{16,24},{20,28},{24,16},{28,20},{1,9},{5... | collective-permute-start | bytes 680 | tf_op jit(solution)/shard_map/while/body/eval_jaxpr/ppermute | solution.py:59
  80.8 3.6 %collective-permute-start.2 = (f32[8,7]{0,1:T(8,128)S(1)}, f32[8,7]{0,1:T(8,128)S(1)}, u32[]{:S(2)}, u32[]{:S(2)}) collective-permute-start(f32[8,7]{0,1:T(8,128)S(1)} %add.81), channel_id=1, source_target_pairs={{0,16},{4,20},{8,24},{12,28},{16,0},{20,4},{24,8},{28,12},{1,17},{... | collective-permute-start | bytes 680 | tf_op jit(solution)/shard_map/while/body/eval_jaxpr/ppermute | solution.py:59
  84.8 1.2 %collective-permute-start = (f32[8,7]{0,1:T(8,128)S(1)}, f32[8,7]{0,1:T(8,128)S(1)}, u32[]{:S(2)}, u32[]{:S(2)}) collective-permute-start(f32[8,7]{0,1:T(8,128)S(1)} %select_reduce_fusion.2), channel_id=1, source_target_pairs={{0,4},{4,0},{8,12},{12,8},{16,20},{20,16},{24,28},{28,24},{1,5},{5... | collective-permute-start | bytes 680 | tf_op jit(solution)/shard_map/while/body/eval_jaxpr/ppermute | solution.py:59
  86.0 3.6 %collective-permute-start.1 = (f32[8,7]{0,1:T(8,128)S(1)}, f32[8,7]{0,1:T(8,128)S(1)}, u32[]{:S(2)}, u32[]{:S(2)}) collective-permute-start(f32[8,7]{0,1:T(8,128)S(1)} %add.80), channel_id=1, source_target_pairs={{0,8},{4,12},{8,0},{12,4},{16,24},{20,28},{24,16},{28,20},{1,9},{5... | collective-permute-start | bytes 680 | tf_op jit(solution)/shard_map/while/body/eval_jaxpr/ppermute | solution.py:59
  89.6 3.6 %collective-permute-start.2 = (f32[8,7]{0,1:T(8,128)S(1)}, f32[8,7]{0,1:T(8,128)S(1)}, u32[]{:S(2)}, u32[]{:S(2)}) collective-permute-start(f32[8,7]{0,1:T(8,128)S(1)} %add.81), channel_id=1, source_target_pairs={{0,16},{4,20},{8,24},{12,28},{16,0},{20,4},{24,8},{28,12},{1,17},{... | collective-permute-start | bytes 680 | tf_op jit(solution)/shard_map/while/body/eval_jaxpr/ppermute | solution.py:59
Sparse Core Ops, SparseCore 0:
  21.8 19.6 reduce-scatter.1
